TPU v7x, 32 devices: a whole 2x2x4 slice. The times are simulated.
32 devices in a mesh: morton: 16 (over z, y, x), dp: 2 (over core).
Axes of the slice: x: 2, y: 2, z: 4, core: 2. Of those that a mesh axis runs over, the one named last changes fastest.
Arguments:
- node_feat: bfloat16 [2, 8192, 128], P('dp', 'morton'), may hold values from -6 to 6
- edge_feat: bfloat16 [2, 32768, 128], P('dp', 'morton'), may hold values from -6 to 6
- cot_node: bfloat16 [2, 8192, 128], P('dp', 'morton'), may hold values from -6 to 6
- cot_edge: bfloat16 [2, 32768, 128], P('dp', 'morton'), may hold values from -6 to 6
- senders: int32 [2, 32768], P('dp', 'morton'), may hold values from 0 to 767, as said below
- receivers: int32 [2, 32768], P('dp', 'morton'), may hold values from 0 to 511
- send_rows: int32 [2, 4096], P('dp', 'morton'), may hold values from 0 to 511
- edge_count: int32 [2, 16], P('dp', 'morton'), may hold values from 512 to 2048, as said below
- edge_w1: float32 [384, 128], replicated, may hold values from -0.3125 to 0.3125
- edge_w2: float32 [128, 128], replicated, may hold values from -0.5 to 0.5
- edge_gain: float32 [128], replicated, may hold values from 0.25 to 1.75
- node_w1: float32 [256, 128], replicated, may hold values from -0.375 to 0.375
- node_w2: float32 [128, 128], replicated, may hold values from -0.5 to 0.5
- node_gain: float32 [128], replicated, may hold values from 0.25 to 1.75
Outputs:
- grad_node: float32 [2, 8192, 128], P('dp', 'morton')
- grad_edge: float32 [2, 32768, 128], P('dp', 'morton')
- grad_edge_w1: float32 [384, 128], replicated
- grad_edge_w2: float32 [128, 128], replicated
- grad_edge_gain: float32 [128], replicated
- grad_node_w1: float32 [256, 128], replicated
- grad_node_w2: float32 [128, 128], replicated
- grad_node_gain: float32 [128], replicated
Inputs may be any that keep to these rules, and one draw needn't show every extreme that they name: `senders`: on device m, an entry below 512 is one of its own cells; an entry 512 + k * 64 + q is ghost row q of group k, which comes from device m - d_k with d = (-16/2, -1, +1, +16/2); that device always exists. `send_rows`: entry k * 64 + q of device m is its local cell sent to device m + d_k, with d = (-16/2, -1, +1, +16/2). `edge_count`: edge slots at or beyond the count are empty; some device of every block is full.
All inputs are finite; a program needn't handle non-finite values.
Results may differ from a plain program's by a relative error of at most 0.014.
Values may be sent and summed in bfloat16 or wider, within the bound.
No kernel may reach another device: no remote copies, remote signals or barrier semaphores. Data moves between devices by JAX's collectives and lax.ppermute only.
A program may use at most 64 MiB of HBM per device.

v0:
```python
import jax
import jax.numpy as jnp
from jax import lax
from jax.sharding import PartitionSpec as P


def layer_norm(values, gain):
    center = values - jnp.mean(values, axis=-1, keepdims=True)
    spread = jnp.mean(center * center, axis=-1, keepdims=True)
    return center * lax.rsqrt(spread + 1e-05) * gain


def local_forward(
    cells, ghosts, edges, ew1, ew2, egain, nw1, nw2, ngain, sending, receiving, count
):
    table = jnp.concatenate([cells, ghosts], axis=0)
    joined = jnp.concatenate(
        [
            edges.astype(jnp.bfloat16),
            table[sending].astype(jnp.bfloat16),
            cells[receiving].astype(jnp.bfloat16),
        ],
        axis=1,
    )
    first = jnp.dot(joined, ew1.astype(jnp.bfloat16), preferred_element_type=jnp.float32)
    second = jnp.dot(
        jax.nn.silu(first).astype(jnp.bfloat16),
        ew2.astype(jnp.bfloat16),
        preferred_element_type=jnp.float32,
    )
    live = (jnp.arange(edges.shape[0]) < count).astype(edges.dtype)[:, None]
    edge_new = edges + live * layer_norm(second, egain)
    message = (live * edge_new).astype(jnp.bfloat16)
    gathered = jax.ops.segment_sum(
        message.astype(edges.dtype), receiving, num_segments=cells.shape[0]
    )
    stacked = jnp.concatenate([cells.astype(jnp.bfloat16), gathered.astype(jnp.bfloat16)], axis=1)
    hidden = jnp.dot(stacked, nw1.astype(jnp.bfloat16), preferred_element_type=jnp.float32)
    output = jnp.dot(
        jax.nn.silu(hidden).astype(jnp.bfloat16),
        nw2.astype(jnp.bfloat16),
        preferred_element_type=jnp.float32,
    )
    return (cells + layer_norm(output, ngain), edge_new)


def on_device(
    node_feat,
    edge_feat,
    cot_node,
    cot_edge,
    senders,
    receivers,
    send_rows,
    edge_count,
    edge_w1,
    edge_w2,
    edge_gain,
    node_w1,
    node_w2,
    node_gain,
):
    peers = lax.axis_size("morton")
    rank = lax.axis_index("morton")
    offsets = (-(peers // 2), -1, 1, peers // 2)
    width = node_feat.shape[2]
    quota = send_rows.shape[1] // 4
    outgoing = send_rows[0].reshape(4, quota)
    cells_bf = node_feat[0]
    picked = [cells_bf[outgoing[k]] for k in range(4)]
    arrived = []
    buffer = jnp.zeros((peers, quota, width), jnp.bfloat16)
    for k in range(4):
        target = jax.nn.one_hot(rank + offsets[k], peers, dtype=jnp.bfloat16)
        buffer = buffer + target[:, None, None] * picked[k][None]
    received = lax.all_to_all(buffer, "morton", split_axis=0, concat_axis=0, tiled=True)
    for k in range(4):
        source = rank - offsets[k]
        valid = ((source >= 0) & (source < peers)).astype(jnp.float32)
        arrived.append(received[jnp.clip(source, 0, peers - 1)].astype(jnp.float32) * valid)
    ghosts = jnp.concatenate(arrived, axis=0)
    cells = cells_bf.astype(jnp.float32)
    edges = edge_feat[0].astype(jnp.float32)
    sending = senders[0]
    receiving = receivers[0]
    count = edge_count[0, 0]

    def forward(cells, ghosts, edges, ew1, ew2, egain, nw1, nw2, ngain):
        return local_forward(
            cells, ghosts, edges, ew1, ew2, egain, nw1, nw2, ngain, sending, receiving, count
        )

    outputs, pullback = jax.vjp(
        forward, cells, ghosts, edges, edge_w1, edge_w2, edge_gain, node_w1, node_w2, node_gain
    )
    grads = pullback((cot_node[0].astype(jnp.float32), cot_edge[0].astype(jnp.float32)))
    grad_cells = grads[0]
    ghost_grads = grads[1].reshape(4, quota, width)
    buffer = jnp.zeros((peers, quota, width), jnp.float32)
    for k in range(4):
        target = jax.nn.one_hot(rank - offsets[k], peers, dtype=jnp.float32)
        buffer = buffer + target[:, None, None] * ghost_grads[k][None]
    returned = lax.all_to_all(
        buffer.astype(jnp.bfloat16), "morton", split_axis=0, concat_axis=0, tiled=True
    ).astype(buffer.dtype)
    for k in range(4):
        reader = rank + offsets[k]
        valid = ((reader >= 0) & (reader < peers)).astype(jnp.float32)
        grad_cells = grad_cells.at[outgoing[k]].add(
            returned[jnp.clip(reader, 0, peers - 1)] * valid
        )
    summed = lax.psum(
        (grads[3], grads[4], grads[5], grads[6], grads[7], grads[8]), ("morton", "dp")
    )
    factor = 1.0 / jnp.sqrt(jnp.float32(lax.axis_size("dp") * peers * edge_feat.shape[1]))
    return (
        grad_cells[None],
        grads[2][None],
        summed[0] * factor,
        summed[1] * factor,
        summed[2] * factor,
        summed[3] * factor,
        summed[4] * factor,
        summed[5] * factor,
    )


def solution(mesh):
    in_specs = (
        P("dp", "morton", None),
        P("dp", "morton", None),
        P("dp", "morton", None),
        P("dp", "morton", None),
        P("dp", "morton"),
        P("dp", "morton"),
        P("dp", "morton"),
        P("dp", "morton"),
        P(),
        P(),
        P(),
        P(),
        P(),
        P(),
    )
    out_specs = (P("dp", "morton", None), P("dp", "morton", None), P(), P(), P(), P(), P(), P())
    return jax.shard_map(
        on_device, mesh=mesh, in_specs=in_specs, out_specs=out_specs, check_vma=False
    )
```

profile of v0, /device:TPU:1, one launch (start us, length us, event | category | flops | bytes accessed | tf_op | source)
XLA Modules:
  0.0 282.5 jit_solution(1534379466530907861)
XLA Ops:
  8.6 1.5 gather_fusion.3
  10.2 1.5 gather_fusion.1
  11.7 1.5 gather_fusion.2
  13.2 1.5 gather_fusion
  15.6 7.5 %all-to-all-start = ((bf16[16,64,128]{2,1,0:T(8,128)(2,1)}), bf16[16,64,128]{2,1,0:T(8,128)(2,1)S(1)}, u32[]{:S(2)}, u32[]{:S(2)}) async-start(bf16[16,64,128]{2,1,0:T(8,128)(2,1)} %multiply_add_fusion), calls=%async_computation | async-start | bytes 524288 | tf_op jit(solution)/shard_map/all_to_all | solution.py:76
  23.7 1.3 and_reduce_fusion
  29.0 6.2 %gather_fusion.5 = bf16[2048,128]{1,0:T(8,128)(2,1)S(1)} fusion(bf16[512,128]{1,0:T(8,128)(2,1)S(1)} %bitcast.84, s32[2048]{0:T(1024)S(1)} %get-tuple-element.56), kind=kCustom, calls=%fused_computation.5 | custom fusion | bytes 1056768 | tf_op jit(solution)/shard_map/jvp()/gather | solution.py:21
  35.5 6.2 %gather_fusion.4 = bf16[2048,128]{1,0:T(8,128)(2,1)S(1)} fusion(bf16[768,128]{1,0:T(8,128)(2,1)S(1)} %bitcast_dynamic-update-slice_fusion, s32[2048]{0:T(1024)S(1)} %broadcast_clamp_fusion.2), kind=kCustom, calls=%fused_computation.4 | custom fusion | bytes 1056768 | tf_op jit(solution)/shard_map/jvp()/gather | solution.py:20
  45.5 1.3 copy.45
  46.8 12.1 %scatter_custom_fusion = f32[512,128]{1,0:T(8,128)S(1)} fusion(s32[2048]{0:T(1024)} %bitcast.91, f32[2048,128]{1,0:T(8,128)} %copy.45, f32[]{:T(128)} %constant.24.clone.1), kind=kCustom, calls=%fused_computation.77 | custom fusion | flops 262144 | bytes 262656 | tf_op jit(solution)/shard_map/jvp()/scatter-add | solution.py:34
  59.2 1.2 fusion.76
  61.2 0.9 fusion.5
  64.5 6.2 %gather_fusion.6 = bf16[2048,128]{1,0:T(8,128)(2,1)S(1)} fusion(bf16[512,128]{1,0:T(8,128)(2,1)S(1)} %copy.48, s32[2048]{0:T(1024)S(1)} %copy-done.21), kind=kCustom, calls=%fused_computation.6 | custom fusion | bytes 1056768 | tf_op jit(solution)/shard_map/transpose(jvp())/gather | solution.py:34
  72.9 1.1 fusion.4
  75.2 1.2 fusion.2
  76.4 1.5 convolution_convert_fusion
  78.4 1.3 copy.51
  79.8 12.0 %scatter_custom_fusion.1 = f32[768,128]{1,0:T(8,128)S(1)} fusion(s32[2048]{0:T(1024)} %bitcast.94, f32[2048,128]{1,0:T(8,128)} %copy.51, f32[]{:T(128)} %constant.24.clone.1), kind=kCustom, calls=%fused_computation.71 | custom fusion | flops 262144 | bytes 393728 | tf_op jit(solution)/shard_map/transpose(jvp())/scatter-add | solution.py:20
  92.7 40.0 %all-reduce = (f32[128]{0:T(128)S(1)}, f32[128]{0:T(128)S(1)}) all-reduce(f32[128]{0:T(128)S(1)} %get-tuple-element.24, f32[128]{0:T(128)S(1)} %copy-done.35), channel_id=1, replica_groups=mesh['morton'=16,'dp'=2] {'morton','dp'}, use_global_device_ids=true, to_apply=%region_18.19 | all-reduce | flops 256 | bytes 2048 | tf_op jit(solution)/shard_map/psum | solution.py:112
  132.8 0.9 add_convert_fusion
  134.2 1.3 copy.55
  136.6 5.2 %all-to-all-start.1 = ((bf16[16,64,128]{2,1,0:T(8,128)(2,1)}), bf16[16,64,128]{2,1,0:T(8,128)(2,1)S(1)}, u32[]{:S(2)}, u32[]{:S(2)}) async-start(bf16[16,64,128]{2,1,0:T(8,128)(2,1)} %add_convert_fusion), calls=%async_computation.1 | async-start | bytes 524288 | tf_op jit(solution)/shard_map/all_to_all | solution.py:103
  141.8 11.6 %scatter_fusion = f32[512,128]{1,0:T(8,128)S(1)} fusion(f32[512,128]{1,0:T(8,128)S(1)} %copy.53, s32[2048]{0:T(1024)S(1)} %bitcast.90, f32[2048,128]{1,0:T(8,128)S(1)} %copy.54), kind=kCustom, calls=%fused_computation.9 | custom fusion | flops 262144 | bytes 3153920 | tf_op jit(solution)/shard_map/transpose(jvp())/scatter-add | solution.py:21
  153.9 110.2 %all-reduce.4.cloned.1.call-done = (f32[384,128]{1,0:T(8,128)}, f32[128,128]{1,0:T(8,128)}, f32[256,128]{1,0:T(8,128)}, f32[128,128]{1,0:T(8,128)}) async-done(((f32[384,128]{1,0:T(8,128)}, f32[128,128]{1,0:T(8,128)}, f32[256,128]{1,0:T(8,128)}, f32[128,128]{1,0:T(8,128)}), (f32[384,128]{1,0:T(8,128)}, f32[128,128]{1,0:T(8,128)}, f32[256,128]{1,0:T(8,128)}, ...) | async-done | bytes 458768 | tf_op jit(solution)/shard_map/psum | solution.py:112
  264.1 1.5 broadcast_multiply_fusion.3
  265.5 1.5 broadcast_multiply_fusion.2
  267.0 1.6 broadcast_multiply_fusion.1
  268.6 1.6 broadcast_multiply_fusion
  270.2 1.2 scatter_custom_fusion.3
  271.4 1.2 scatter_custom_fusion.4
  272.6 1.2 scatter_custom_fusion.5
  273.7 1.2 scatter_custom_fusion.6
  (144 shorter events, 21.0 us)
Async XLA Ops:
  7.2 20.0 %copy-start.20 = (s32[1,2048]{1,0:T(1,128)S(1)}, s32[1,2048]{1,0:T(1,128)}, u32[]{:S(2)}) copy-start(s32[1,2048]{1,0:T(1,128)} %param.19) | copy-start | bytes 24580
  7.2 21.2 %copy-start.15 = (bf16[1,512,128]{2,1,0:T(8,128)(2,1)S(1)}, bf16[1,512,128]{2,1,0:T(8,128)(2,1)}, u32[]{:S(2)}) copy-start(bf16[1,512,128]{2,1,0:T(8,128)(2,1)} %param.16) | copy-start | bytes 393220
  7.2 21.3 %copy-start.5 = (bf16[1,2048,128]{2,1,0:T(8,128)(2,1)S(1)}, bf16[1,2048,128]{2,1,0:T(8,128)(2,1)}, u32[]{:S(2)}) copy-start(bf16[1,2048,128]{2,1,0:T(8,128)(2,1)} %param.17) | copy-start | bytes 1572868
  7.2 21.5 %copy-start.6 = (bf16[1,2048,128]{2,1,0:T(8,128)(2,1)S(1)}, bf16[1,2048,128]{2,1,0:T(8,128)(2,1)}, u32[]{:S(2)}) copy-start(bf16[1,2048,128]{2,1,0:T(8,128)(2,1)} %param.15) | copy-start | bytes 1572868
  8.1 3.6 %copy-start.31 = (s32[64]{0:T(128)}, s32[64]{0:T(128)S(1)}, u32[]{:S(2)}) copy-start(s32[64]{0:T(128)S(1)} %get-tuple-element.49) | copy-start | bytes 772
  8.1 3.6 %copy-start.32 = (s32[64]{0:T(128)}, s32[64]{0:T(128)S(1)}, u32[]{:S(2)}) copy-start(s32[64]{0:T(128)S(1)} %get-tuple-element.50) | copy-start | bytes 772
  15.6 13.3 %copy-start.1 = (bf16[1,512,128]{2,1,0:T(8,128)(2,1)S(1)}, bf16[1,512,128]{2,1,0:T(8,128)(2,1)}, u32[]{:S(2)}) copy-start(bf16[1,512,128]{2,1,0:T(8,128)(2,1)} %param.14) | copy-start | bytes 393220
  15.6 19.8 %all-to-all-start = ((bf16[16,64,128]{2,1,0:T(8,128)(2,1)}), bf16[16,64,128]{2,1,0:T(8,128)(2,1)S(1)}, u32[]{:S(2)}, u32[]{:S(2)}) async-start(bf16[16,64,128]{2,1,0:T(8,128)(2,1)} %multiply_add_fusion), calls=%async_computation | async-start | bytes 524288 | tf_op jit(solution)/shard_map/all_to_all | solution.py:76
  23.2 240.9 %all-reduce.4.cloned.1.call-start = ((), (), s32[]{:S(2)}) async-start(), calls=%async_computation.2 | async-start | bytes 917504 | tf_op jit(solution)/shard_map/psum | solution.py:112
  25.8 2.6 copy-start.18
  27.1 8.2 %copy-start.22 = (s32[2048,1]{0,1:T(1,128)}, s32[2048,1]{0,1:T(1,128)S(1)}, u32[]{:S(2)}) copy-start(s32[2048,1]{0,1:T(1,128)S(1)} %compare_select_fusion.1) | copy-start | bytes 24580
  35.4 6.6 %copy-start.7 = (bf16[2048,128]{0,1:T(8,128)(2,1)}, bf16[2048,128]{0,1:T(8,128)(2,1)S(1)}, u32[]{:S(2)}) copy-start(bf16[2048,128]{0,1:T(8,128)(2,1)S(1)} %copy.44) | copy-start | bytes 1572868
  35.5 6.4 %copy-start.12 = (f32[384,128]{1,0:T(8,128)S(1)}, f32[384,128]{1,0:T(8,128)}, u32[]{:S(2)}) copy-start(f32[384,128]{1,0:T(8,128)} %param.22) | copy-start | bytes 589828
  42.9 2.3 copy-start.24
  45.5 13.4 %copy-start.11 = (f32[256,128]{1,0:T(8,128)S(1)}, f32[256,128]{1,0:T(8,128)}, u32[]{:S(2)}) copy-start(f32[256,128]{1,0:T(8,128)} %param.25) | copy-start | bytes 393220
  46.8 13.5 %copy-start.26 = (f32[128]{0:T(128)S(1)}, f32[128]{0:T(128)}, u32[]{:S(2)}) copy-start(f32[128]{0:T(128)} %param.27) | copy-start | bytes 1540
  59.2 2.9 %copy-start.36 = (f32[128,128]{1,0:T(8,128)S(1)}, f32[128,128]{1,0:T(8,128)}, u32[]{:S(2)}) copy-start(f32[128,128]{1,0:T(8,128)} %param.26) | copy-start | bytes 196612
  62.1 2.3 copy-start.21
  64.4 6.4 %copy-start.14 = (f32[2048]{0:T(1024)S(1)}, f32[2048]{0:T(1024)}, u32[]{:S(2)}) copy-start(f32[2048]{0:T(1024)} %copy-done.13) | copy-start | bytes 24580
  64.5 6.4 %copy-start.23 = (pred[2048]{0:T(1024)(128)(4,1)S(1)}, pred[2048]{0:T(1024)(128)(4,1)}, u32[]{:S(2)}) copy-start(pred[2048]{0:T(1024)(128)(4,1)} %and_reduce_fusion) | copy-start | bytes 6148
  64.5 6.4 %copy-start.25 = (f32[128]{0:T(128)S(1)}, f32[128]{0:T(128)}, u32[]{:S(2)}) copy-start(f32[128]{0:T(128)} %param.24) | copy-start | bytes 1540
  71.6 1.2 copy-start.40
  72.9 1.1 copy-start.38
  74.0 1.2 copy-start.10
  79.7 12.2 %copy-start.4 = (bf16[512,256]{0,1:T(8,128)(2,1)S(1)}, bf16[512,256]{0,1:T(8,128)(2,1)}, u32[]{:S(2)}) copy-start(bf16[512,256]{0,1:T(8,128)(2,1)} %copy-done.3) | copy-start | bytes 786436
  79.7 13.0 %copy-start.35 = (f32[128]{0:T(128)S(1)}, f32[128]{0:T(128)}, u32[]{:S(2)}) copy-start(f32[128]{0:T(128)} %get-tuple-element.26) | copy-start | bytes 1540
  79.7 53.0 %copy-start.27 = (f32[16]{0:T(128)S(1)}, f32[16]{0:T(128)}, u32[]{:S(2)}) copy-start(f32[16]{0:T(128)} %get-tuple-element.67) | copy-start | bytes 196
  79.7 53.0 %copy-start.28 = (f32[16]{0:T(128)S(1)}, f32[16]{0:T(128)}, u32[]{:S(2)}) copy-start(f32[16]{0:T(128)} %get-tuple-element.68) | copy-start | bytes 196
  79.7 53.0 %copy-start.29 = (f32[16]{0:T(128)S(1)}, f32[16]{0:T(128)}, u32[]{:S(2)}) copy-start(f32[16]{0:T(128)} %get-tuple-element.65) | copy-start | bytes 196
  79.7 53.0 %copy-start.30 = (f32[16]{0:T(128)S(1)}, f32[16]{0:T(128)}, u32[]{:S(2)}) copy-start(f32[16]{0:T(128)} %get-tuple-element.66) | copy-start | bytes 196
  135.5 6.2 %copy-start.19 = (s32[2048,1]{0,1:T(1,128)S(1)}, s32[2048,1]{0,1:T(1,128)}, u32[]{:S(2)}) copy-start(s32[2048,1]{0,1:T(1,128)} %copy-done.18) | copy-start | bytes 24580
  136.6 133.6 %all-to-all-start.1 = ((bf16[16,64,128]{2,1,0:T(8,128)(2,1)}), bf16[16,64,128]{2,1,0:T(8,128)(2,1)S(1)}, u32[]{:S(2)}, u32[]{:S(2)}) async-start(bf16[16,64,128]{2,1,0:T(8,128)(2,1)} %add_convert_fusion), calls=%async_computation.1 | async-start | bytes 524288 | tf_op jit(solution)/shard_map/all_to_all | solution.py:103
  (12 other events, 9.0 us)
Sparse Core Ops, SparseCore 0:
  132.9 131.1 all-reduce.3
where the time goes:
time: 284 us; the launch traced here: 282 us
  waiting for transfers between devices  110 us (39%)
  other arithmetic  58.2 us (20%)
  blocking collectives  40 us (14%)
  local copies, waits for them, and re-layouts  36.5 us (13%)
  between operations  15.4 us (5%)
  starting transfers between devices  12.7 us (4%)
  matrix products  9.35 us (3%)
    psum x1, waiting for transfers between devices, on_device(): lax.psum((grads[3], grads[4], grads[5], grads[6], grads[7], grads[8]), ('...  110 us
    psum x1, blocking collectives, on_device(): lax.psum((grads[3], grads[4], grads[5], grads[6], grads[7], grads[8]), ('...  40 us
    scatter-add x1, other arithmetic, local_forward(): jax.ops.segment_sum(message.astype(edges.dtype), receiving, num_segments=...  12.1 us
    scatter-add x1, other arithmetic, local_forward(): table[sending].astype(jnp.bfloat16)  12 us
    scatter-add x1, other arithmetic, local_forward(): cells[receiving].astype(jnp.bfloat16)  11.6 us
    unnamed x87, local copies, waits for them, and re-layouts  8.03 us
    all_to_all x1, starting transfers between devices, on_device(): lax.all_to_all(buffer, 'morton', split_axis=0, concat_axis=0, tiled=True)  7.53 us
    gather x2, local copies, waits for them, and re-layouts, local_forward(): cells[receiving].astype(jnp.bfloat16)  6.4 us
  transfers between devices with their start and end apart: 3, of which 1 were waited for; matrix products, arithmetic and copies ran while one was open for 12% of the time, Pallas kernels for 0%

commit v1 on v0

--- a/solution.py
+++ b/solution.py
@@ -109,9 +109,9 @@
         grad_cells = grad_cells.at[outgoing[k]].add(
             returned[jnp.clip(reader, 0, peers - 1)] * valid
         )
-    summed = lax.psum(
-        (grads[3], grads[4], grads[5], grads[6], grads[7], grads[8]), ("morton", "dp")
-    )
+    summed = (grads[3], grads[4], grads[5], grads[6], grads[7], grads[8])
+    for mesh_axis in ("dp", "morton"):
+        summed = lax.psum(summed, mesh_axis)
     factor = 1.0 / jnp.sqrt(jnp.float32(lax.axis_size("dp") * peers * edge_feat.shape[1]))
     return (
         grad_cells[None],

time: 284 us -> 258 us (0.908)
  waiting for transfers between devices: 110 us -> 81 us
  other arithmetic: 58.2 us -> 61.7 us
    psum x1 -> x2, waiting for transfers between devices: 110 us -> 80.3 us  [on_device(): summed = lax.psum(summed, mesh_axis)]
    psum x1 -> x2, blocking collectives: 40 us -> 37.3 us  [on_device(): summed = lax.psum(summed, mesh_axis)]
    unnamed x87 -> x93, local copies, waits for them, and re-layouts: 8.03 us -> 8.04 us
  transfers between devices with their start and end apart: 3 -> 4, of which waited for: 1 -> 2; matrix products, arithmetic and copies ran while one was open for 12% -> 13% of each run, Pallas kernels for 0% -> 0%
where the time goes in v1:
time: 258 us; the launch traced here: 255 us
  waiting for transfers between devices  81 us (31%)
  other arithmetic  61.7 us (24%)
  blocking collectives  37.3 us (14%)
  local copies, waits for them, and re-layouts  37.2 us (14%)
  between operations  15.4 us (6%)
  starting transfers between devices  14 us (5%)
  matrix products  8.4 us (3%)
    psum x2, waiting for transfers between devices, on_device(): summed = lax.psum(summed, mesh_axis)  80.3 us
    psum x2, blocking collectives, on_device(): summed = lax.psum(summed, mesh_axis)  37.3 us
    scatter-add x1, other arithmetic, local_forward(): jax.ops.segment_sum(message.astype(edges.dtype), receiving, num_segments=...  12.1 us
    scatter-add x1, other arithmetic, local_forward(): table[sending].astype(jnp.bfloat16)  12 us
    scatter-add x1, other arithmetic, local_forward(): cells[receiving].astype(jnp.bfloat16)  11.6 us
    unnamed x93, local copies, waits for them, and re-layouts  8.04 us
    all_to_all x1, starting transfers between devices, on_device(): lax.all_to_all(buffer, 'morton', split_axis=0, concat_axis=0, tiled=True)  7.53 us
    all_to_all x1, starting transfers between devices, on_device(): lax.all_to_all(buffer.astype(jnp.bfloat16), 'morton', split_axis=0, conca...  6.4 us
  transfers between devices with their start and end apart: 4, of which 2 were waited for; matrix products, arithmetic and copies ran while one was open for 13% of the time, Pallas kernels for 0%

profile of v1, /device:TPU:1, one launch (start us, length us, event | category | flops | bytes accessed | tf_op | source)
XLA Modules:
  0.0 255.1 jit_solution(17952820715654709720)
XLA Ops:
  8.7 1.5 gather_fusion.3
  10.2 1.5 gather_fusion.1
  11.8 1.5 gather_fusion.2
  13.3 1.5 gather_fusion
  15.7 7.5 %all-to-all-start = ((bf16[16,64,128]{2,1,0:T(8,128)(2,1)}), bf16[16,64,128]{2,1,0:T(8,128)(2,1)S(1)}, u32[]{:S(2)}, u32[]{:S(2)}) async-start(bf16[16,64,128]{2,1,0:T(8,128)(2,1)} %multiply_add_fusion), calls=%async_computation | async-start | bytes 524288 | tf_op jit(solution)/shard_map/all_to_all | solution.py:76
  23.8 1.3 and_reduce_fusion
  29.0 6.2 %gather_fusion.5 = bf16[2048,128]{1,0:T(8,128)(2,1)S(1)} fusion(bf16[512,128]{1,0:T(8,128)(2,1)S(1)} %bitcast.84, s32[2048]{0:T(1024)S(1)} %get-tuple-element.62), kind=kCustom, calls=%fused_computation.5 | custom fusion | bytes 1056768 | tf_op jit(solution)/shard_map/jvp()/gather | solution.py:21
  35.6 6.2 %gather_fusion.4 = bf16[2048,128]{1,0:T(8,128)(2,1)S(1)} fusion(bf16[768,128]{1,0:T(8,128)(2,1)S(1)} %bitcast_dynamic-update-slice_fusion, s32[2048]{0:T(1024)S(1)} %broadcast_clamp_fusion.2), kind=kCustom, calls=%fused_computation.4 | custom fusion | bytes 1056768 | tf_op jit(solution)/shard_map/jvp()/gather | solution.py:20
  45.6 1.3 copy.45
  46.9 12.1 %scatter_custom_fusion = f32[512,128]{1,0:T(8,128)S(1)} fusion(s32[2048]{0:T(1024)} %bitcast.91, f32[2048,128]{1,0:T(8,128)} %copy.45, f32[]{:T(128)} %constant.24.clone.1), kind=kCustom, calls=%fused_computation.77 | custom fusion | flops 262144 | bytes 262656 | tf_op jit(solution)/shard_map/jvp()/scatter-add | solution.py:34
  64.6 6.2 %gather_fusion.6 = bf16[2048,128]{1,0:T(8,128)(2,1)S(1)} fusion(bf16[512,128]{1,0:T(8,128)(2,1)S(1)} %copy.48, s32[2048]{0:T(1024)S(1)} %copy-done.25), kind=kCustom, calls=%fused_computation.6 | custom fusion | bytes 1056768 | tf_op jit(solution)/shard_map/transpose(jvp())/gather | solution.py:34
  75.8 1.2 fusion.2
  77.7 1.2 slice_convert_fusion
  78.9 1.3 copy.51
  80.2 12.0 %scatter_custom_fusion.1 = f32[768,128]{1,0:T(8,128)S(1)} fusion(s32[2048]{0:T(1024)} %bitcast.94, f32[2048,128]{1,0:T(8,128)} %copy.51, f32[]{:T(128)} %constant.24.clone.1), kind=kCustom, calls=%fused_computation.71 | custom fusion | flops 262144 | bytes 393728 | tf_op jit(solution)/shard_map/transpose(jvp())/scatter-add | solution.py:20
  94.0 1.6 add_convert_fusion
  95.6 6.4 %all-to-all-start.1 = ((bf16[16,64,128]{2,1,0:T(8,128)(2,1)}), bf16[16,64,128]{2,1,0:T(8,128)(2,1)}, u32[]{:S(2)}, u32[]{:S(2)}) async-start(bf16[16,64,128]{2,1,0:T(8,128)(2,1)} %add_convert_fusion), calls=%async_computation.1 | async-start | bytes 524288 | tf_op jit(solution)/shard_map/all_to_all | solution.py:103
  102.8 1.2 add_bitcast_fusion
  104.0 23.2 %all-reduce.9.cloned.1.call-done = (f32[384,128]{1,0:T(8,128)}, f32[128,128]{1,0:T(8,128)}, f32[256,128]{1,0:T(8,128)}, f32[128,128]{1,0:T(8,128)}) async-done(((f32[384,128]{1,0:T(8,128)}, f32[128,128]{1,0:T(8,128)}, f32[256,128]{1,0:T(8,128)}, f32[128,128]{1,0:T(8,128)}), (f32[384,128]{1,0:T(8,128)}, f32[128,128]{1,0:T(8,128)}, f32[256,128]{1,0:T(8,128)}, ...) | async-done | bytes 458768 | tf_op jit(solution)/shard_map/psum | solution.py:114
  127.3 1.3 copy.55
  129.3 11.6 %scatter_fusion = f32[512,128]{1,0:T(8,128)S(1)} fusion(f32[512,128]{1,0:T(8,128)S(1)} %copy.53, s32[2048]{0:T(1024)S(1)} %bitcast.90, f32[2048,128]{1,0:T(8,128)S(1)} %copy.54), kind=kCustom, calls=%fused_computation.9 | custom fusion | flops 262144 | bytes 3153920 | tf_op jit(solution)/shard_map/transpose(jvp())/scatter-add | solution.py:21
  140.9 2.5 all-reduce.2
  143.4 34.9 %all-reduce = (f32[128]{0:T(128)S(1)}, f32[128]{0:T(128)S(1)}) all-reduce(f32[128]{0:T(128)S(1)} %get-tuple-element.36, f32[128]{0:T(128)S(1)} %get-tuple-element.37), channel_id=1, replica_groups=mesh['morton'=16,'dp'=2] {'morton'}, use_global_device_ids=true, to_apply=%region_21.22 | all-reduce | flops 256 | bytes 2048 | tf_op jit(solution)/shard_map/psum | solution.py:114
  180.3 1.2 scatter_custom_fusion.3
  181.5 1.2 scatter_custom_fusion.4
  182.7 1.2 scatter_custom_fusion.5
  183.8 1.2 scatter_custom_fusion.6
  185.0 57.1 %all-reduce.7.cloned.1.call-done = (f32[384,128]{1,0:T(8,128)}, f32[128,128]{1,0:T(8,128)}, f32[256,128]{1,0:T(8,128)}, f32[128,128]{1,0:T(8,128)}) async-done(((f32[384,128]{1,0:T(8,128)}, f32[128,128]{1,0:T(8,128)}, f32[256,128]{1,0:T(8,128)}, f32[128,128]{1,0:T(8,128)}), (f32[384,128]{1,0:T(8,128)}, f32[128,128]{1,0:T(8,128)}, f32[256,128]{1,0:T(8,128)}, ...) | async-done | bytes 458768 | tf_op jit(solution)/shard_map/psum | solution.py:114
  242.1 1.6 broadcast_multiply_fusion
  243.7 1.5 broadcast_multiply_fusion.3
  245.2 1.5 broadcast_multiply_fusion.2
  246.7 1.6 broadcast_multiply_fusion.1
  (154 shorter events, 26.5 us)
Async XLA Ops:
  7.2 20.1 %copy-start.24 = (s32[1,2048]{1,0:T(1,128)S(1)}, s32[1,2048]{1,0:T(1,128)}, u32[]{:S(2)}) copy-start(s32[1,2048]{1,0:T(1,128)} %param.19) | copy-start | bytes 24580
  7.2 21.3 %copy-start.19 = (bf16[1,512,128]{2,1,0:T(8,128)(2,1)S(1)}, bf16[1,512,128]{2,1,0:T(8,128)(2,1)}, u32[]{:S(2)}) copy-start(bf16[1,512,128]{2,1,0:T(8,128)(2,1)} %param.16) | copy-start | bytes 393220
  7.2 21.4 %copy-start.8 = (bf16[1,2048,128]{2,1,0:T(8,128)(2,1)S(1)}, bf16[1,2048,128]{2,1,0:T(8,128)(2,1)}, u32[]{:S(2)}) copy-start(bf16[1,2048,128]{2,1,0:T(8,128)(2,1)} %param.17) | copy-start | bytes 1572868
  7.2 21.6 %copy-start.9 = (bf16[1,2048,128]{2,1,0:T(8,128)(2,1)S(1)}, bf16[1,2048,128]{2,1,0:T(8,128)(2,1)}, u32[]{:S(2)}) copy-start(bf16[1,2048,128]{2,1,0:T(8,128)(2,1)} %param.15) | copy-start | bytes 1572868
  8.1 3.6 %copy-start.33 = (s32[64]{0:T(128)}, s32[64]{0:T(128)S(1)}, u32[]{:S(2)}) copy-start(s32[64]{0:T(128)S(1)} %get-tuple-element.55) | copy-start | bytes 772
  8.1 3.6 %copy-start.34 = (s32[64]{0:T(128)}, s32[64]{0:T(128)S(1)}, u32[]{:S(2)}) copy-start(s32[64]{0:T(128)S(1)} %get-tuple-element.56) | copy-start | bytes 772
  15.7 13.4 %copy-start.1 = (bf16[1,512,128]{2,1,0:T(8,128)(2,1)S(1)}, bf16[1,512,128]{2,1,0:T(8,128)(2,1)}, u32[]{:S(2)}) copy-start(bf16[1,512,128]{2,1,0:T(8,128)(2,1)} %param.14) | copy-start | bytes 393220
  15.7 19.8 %all-to-all-start = ((bf16[16,64,128]{2,1,0:T(8,128)(2,1)}), bf16[16,64,128]{2,1,0:T(8,128)(2,1)S(1)}, u32[]{:S(2)}, u32[]{:S(2)}) async-start(bf16[16,64,128]{2,1,0:T(8,128)(2,1)} %multiply_add_fusion), calls=%async_computation | async-start | bytes 524288 | tf_op jit(solution)/shard_map/all_to_all | solution.py:76
  25.8 2.6 %copy-start.22 = (s32[2048,1]{0,1:T(1,128)}, s32[2048,1]{0,1:T(1,128)S(1)}, u32[]{:S(2)}) copy-start(s32[2048,1]{0,1:T(1,128)S(1)} %compare_select_fusion) | copy-start | bytes 24580
  27.2 8.2 %copy-start.26 = (s32[2048,1]{0,1:T(1,128)}, s32[2048,1]{0,1:T(1,128)S(1)}, u32[]{:S(2)}) copy-start(s32[2048,1]{0,1:T(1,128)S(1)} %compare_select_fusion.1) | copy-start | bytes 24580
  35.4 6.6 %copy-start.10 = (bf16[2048,128]{0,1:T(8,128)(2,1)}, bf16[2048,128]{0,1:T(8,128)(2,1)S(1)}, u32[]{:S(2)}) copy-start(bf16[2048,128]{0,1:T(8,128)(2,1)S(1)} %copy.44) | copy-start | bytes 1572868
  35.6 6.4 %copy-start.15 = (f32[384,128]{1,0:T(8,128)S(1)}, f32[384,128]{1,0:T(8,128)}, u32[]{:S(2)}) copy-start(f32[384,128]{1,0:T(8,128)} %param.22) | copy-start | bytes 589828
  43.0 2.3 copy-start.28
  45.6 13.4 %copy-start.14 = (f32[256,128]{1,0:T(8,128)S(1)}, f32[256,128]{1,0:T(8,128)}, u32[]{:S(2)}) copy-start(f32[256,128]{1,0:T(8,128)} %param.25) | copy-start | bytes 393220
  46.9 13.5 %copy-start.30 = (f32[128]{0:T(128)S(1)}, f32[128]{0:T(128)}, u32[]{:S(2)}) copy-start(f32[128]{0:T(128)} %param.27) | copy-start | bytes 1540
  59.2 2.9 %copy-start.39 = (f32[128,128]{1,0:T(8,128)S(1)}, f32[128,128]{1,0:T(8,128)}, u32[]{:S(2)}) copy-start(f32[128,128]{1,0:T(8,128)} %param.26) | copy-start | bytes 196612
  62.2 2.3 copy-start.25
  64.5 6.4 %copy-start.18 = (f32[2048]{0:T(1024)S(1)}, f32[2048]{0:T(1024)}, u32[]{:S(2)}) copy-start(f32[2048]{0:T(1024)} %copy-done.17) | copy-start | bytes 24580
  64.5 6.4 %copy-start.27 = (pred[2048]{0:T(1024)(128)(4,1)S(1)}, pred[2048]{0:T(1024)(128)(4,1)}, u32[]{:S(2)}) copy-start(pred[2048]{0:T(1024)(128)(4,1)} %and_reduce_fusion) | copy-start | bytes 6148
  64.5 6.4 %copy-start.29 = (f32[128]{0:T(128)S(1)}, f32[128]{0:T(128)}, u32[]{:S(2)}) copy-start(f32[128]{0:T(128)} %param.24) | copy-start | bytes 1540
  72.1 1.4 copy-start.43
  78.9 15.1 %copy-start.31 = (f32[16]{0:T(128)S(1)}, f32[16]{0:T(128)}, u32[]{:S(2)}) copy-start(f32[16]{0:T(128)} %get-tuple-element.73) | copy-start | bytes 196
  78.9 15.1 %copy-start.32 = (f32[16]{0:T(128)S(1)}, f32[16]{0:T(128)}, u32[]{:S(2)}) copy-start(f32[16]{0:T(128)} %get-tuple-element.74) | copy-start | bytes 196
  80.2 22.6 %copy-start.3 = (bf16[2048,128]{0,1:T(8,128)(2,1)S(1)}, bf16[2048,128]{0,1:T(8,128)(2,1)}, u32[]{:S(2)}) copy-start(bf16[2048,128]{0,1:T(8,128)(2,1)} %copy-done.2) | copy-start | bytes 1572868
  95.6 83.7 %all-to-all-start.1 = ((bf16[16,64,128]{2,1,0:T(8,128)(2,1)}), bf16[16,64,128]{2,1,0:T(8,128)(2,1)}, u32[]{:S(2)}, u32[]{:S(2)}) async-start(bf16[16,64,128]{2,1,0:T(8,128)(2,1)} %add_convert_fusion), calls=%async_computation.1 | async-start | bytes 524288 | tf_op jit(solution)/shard_map/all_to_all | solution.py:103
  102.0 25.2 %all-reduce.9.cloned.1.call-start = ((), (), s32[]{:S(2)}) async-start(), calls=%async_computation.3 | async-start | bytes 917504 | tf_op jit(solution)/shard_map/psum | solution.py:114
  102.8 24.5 %copy-start.7 = (bf16[512,256]{0,1:T(8,128)(2,1)S(1)}, bf16[512,256]{0,1:T(8,128)(2,1)}, u32[]{:S(2)}) copy-start(bf16[512,256]{0,1:T(8,128)(2,1)} %copy-done.6) | copy-start | bytes 786436
  102.8 139.3 %all-reduce.7.cloned.1.call-start = ((), (), s32[]{:S(2)}) async-start(), calls=%async_computation.2 | async-start | bytes 917504 | tf_op jit(solution)/shard_map/psum | solution.py:114
  104.0 23.3 %copy-start.5 = (f32[1,2048,128]{1,2,0:T(8,128)S(1)}, f32[1,2048,128]{1,2,0:T(8,128)}, u32[]{:S(2)}) copy-start(f32[1,2048,128]{1,2,0:T(8,128)} %add_bitcast_fusion) | copy-start | bytes 3145732
  129.3 11.6 %copy-start.37 = (f32[128]{0:T(128)S(1)}, f32[128]{0:T(128)}, u32[]{:S(2)}) copy-start(f32[128]{0:T(128)} %get-tuple-element.26) | copy-start | bytes 1540
  129.3 11.6 %copy-start.38 = (f32[128]{0:T(128)S(1)}, f32[128]{0:T(128)}, u32[]{:S(2)}) copy-start(f32[128]{0:T(128)} %get-tuple-element.24) | copy-start | bytes 1540
  185.0 63.2 %copy-start = (f32[512,128]{1,0:T(8,128)}, f32[512,128]{1,0:T(8,128)S(1)}, u32[]{:S(2)}) copy-start(f32[512,128]{1,0:T(8,128)S(1)} %scatter_custom_fusion.6) | copy-start | bytes 786436
  (16 other events, 14.4 us)
Sparse Core Ops, SparseCore 0:
  106.0 21.2 all-reduce.8
  132.7 109.2 all-reduce.6
